TPU v7x, 32 devices: a whole 2x2x4 slice. The times are simulated.
32 devices in a mesh: rows: 8 (over z, y), grp: 4 (over x, core).
Axes of the slice: x: 2, y: 2, z: 4, core: 2. Of those that a mesh axis runs over, the one named last changes fastest.
Arguments:
- basis: float32 [32, 65536], P(None, ('rows', 'grp')), may hold values from -0.03125 to 0.03125, as said below
- core: float32 [32, 32], replicated, may hold values from -0.3 to 4
- snapshots: bfloat16 [4, 32, 65536], P(None, 'grp', 'rows'), may hold values from -16 to 16
Outputs:
- new_basis: float32 [32, 65536], P(None, ('rows', 'grp'))
- new_core: float32 [32, 32], replicated
- first_coeffs: float32 [4, 32, 32], replicated
Inputs may be any that keep to these rules, and one draw needn't show every extreme that they name: `basis`: rows orthonormal up to float32 rounding.
All inputs are finite; a program needn't handle non-finite values.
Results may differ from a plain program's by a relative error of at most 0.0003.
Values may be sent and summed in bfloat16 or wider, within the bound.
A program may use at most 64 MiB of HBM per device.

v0:
```python
import jax
import jax.numpy as jnp
from jax import lax
from jax.sharding import PartitionSpec as P

BATCHES = 4
epsilon = 1e-06


def contract_rows(left, right):
    return lax.dot_general(
        left,
        right,
        (((1,), (1,)), ((), ())),
        precision=lax.Precision.HIGHEST,
        preferred_element_type=jnp.float32,
    )


def matmul(left, right):
    return jnp.dot(left, right, precision=lax.Precision.HIGHEST, preferred_element_type=jnp.float32)


def lower_solve(factor, right):
    return lax.linalg.triangular_solve(factor, right, left_side=True, lower=True)


def small_update(core_now, total, lower):
    rank = core_now.shape[0]
    cols = lower.shape[0]
    top = jnp.concatenate([core_now, total], axis=1)
    bottom = jnp.concatenate([jnp.zeros((cols, rank), jnp.float32), lower.T], axis=1)
    stacked = jnp.concatenate([top, bottom], axis=0)
    moment = matmul(stacked, stacked.T)
    leading = moment[:, :rank]
    factor = jnp.linalg.cholesky(matmul(leading.T, leading))
    rotation = lower_solve(factor, leading.T).T
    fresh_core = jnp.linalg.cholesky(matmul(rotation.T, matmul(moment, rotation)))
    return (rotation, fresh_core)


def body(basis, core, snapshots):
    rank = basis.shape[0]
    basis_now = basis
    core_now = core
    firsts = []
    gram_basis = lax.psum(contract_rows(basis_now, basis_now), ("rows", "grp"))
    for batch in range(BATCHES):
        columns = lax.all_to_all(snapshots[batch], "grp", split_axis=1, concat_axis=0, tiled=True)
        raw = columns.astype(jnp.float32)
        raw_cross, raw_gram = lax.psum(
            (contract_rows(basis_now, raw), contract_rows(raw, raw)), ("rows", "grp")
        )
        inverse = lax.rsqrt(jnp.diagonal(raw_gram) + epsilon)
        scaled = raw * inverse[:, None]
        cross = raw_cross * inverse[None, :]
        gram_raw = raw_gram * inverse[:, None] * inverse[None, :]
        second = cross - matmul(gram_basis, cross)
        total = cross + second
        basis_cross = cross - matmul(gram_basis, total)
        gram = (
            gram_raw
            - matmul(total.T, cross)
            - matmul(cross.T, total)
            + matmul(total.T, matmul(gram_basis, total))
        )
        twice = scaled - matmul(total.T, basis_now)
        lower = jnp.linalg.cholesky(gram)
        fresh = lower_solve(lower, twice)
        rotation, core_now = small_update(core_now, total, lower)
        cross_fresh = lower_solve(lower, basis_cross.T).T
        halfway = lower_solve(lower, gram)
        gram_fresh = lower_solve(lower, halfway.T).T
        upper_block = jnp.concatenate([gram_basis, cross_fresh], axis=1)
        lower_block = jnp.concatenate([cross_fresh.T, gram_fresh], axis=1)
        combined = jnp.concatenate([upper_block, lower_block], axis=0)
        gram_basis = matmul(rotation.T, matmul(combined, rotation))
        firsts.append(cross)
        basis_now = matmul(rotation[:rank].T, basis_now) + matmul(rotation[rank:].T, fresh)
    return (basis_now, core_now, jnp.stack(firsts, axis=0))


def solution(mesh):
    return jax.shard_map(
        body,
        mesh=mesh,
        in_specs=(P(None, ("rows", "grp")), P(), P(None, "grp", "rows")),
        out_specs=(P(None, ("rows", "grp")), P(), P()),
        check_vma=False,
    )
```

profile of v0, /device:TPU:0, one launch (start us, length us, event | category | flops | bytes accessed | tf_op | source)
XLA Modules:
  0.0 283.6 jit_solution(1562950860485663812)
XLA Ops:
  0.6 1.9 fusion.229
  2.6 4.4 %all-to-all-start = ((bf16[8,4,2048]{2,0,1:T(8,128)(2,1)}), bf16[8,4,2048]{2,0,1:T(8,128)(2,1)S(1)}, u32[]{:S(2)}, u32[]{:S(2)}) async-start(bf16[8,4,2048]{2,0,1:T(8,128)(2,1)} %bitcast), calls=%async_computation | async-start | bytes 262144 | tf_op jit(solution)/shard_map/all_to_all | solution.py:49
  7.4 4.1 %all-to-all-done = bf16[8,4,2048]{2,0,1:T(8,128)(2,1)S(1)} async-done(((bf16[8,4,2048]{2,0,1:T(8,128)(2,1)}), bf16[8,4,2048]{2,0,1:T(8,128)(2,1)S(1)}, u32[]{:S(2)}, u32[]{:S(2)}) %all-to-all-start) | async-done | bytes 131104 | tf_op jit(solution)/shard_map/all_to_all | solution.py:49
  11.6 3.3 %all-to-all-start.1 = ((bf16[8,4,2048]{2,0,1:T(8,128)(2,1)}), bf16[8,4,2048]{2,0,1:T(8,128)(2,1)S(1)}, u32[]{:S(2)}, u32[]{:S(2)}) async-start(bf16[8,4,2048]{2,0,1:T(8,128)(2,1)} %bitcast.15), calls=%async_computation.1 | async-start | bytes 262144 | tf_op jit(solution)/shard_map/all_to_all | solution.py:49
  15.3 42.1 %all-reduce.7 = (f32[32,32]{1,0:T(8,128)S(1)}, f32[32,32]{0,1:T(8,128)S(1)}, f32[32,32]{0,1:T(8,128)S(1)}) all-reduce(f32[32,32]{1,0:T(8,128)S(1)} %fusion.230, f32[32,32]{0,1:T(8,128)S(1)} %fusion.18, f32[32,32]{0,1:T(8,128)S(1)} %fusion.16), channel_id=1, replica_groups=mesh['rows'=8,'grp'=4] {'rows','grp'}, use_global_device_ids=true, to_apply=%region_2.0 | all-reduce | flops 3072 | bytes 24576 | tf_op jit(solution)/shard_map/psum | solution.py:47
  57.4 0.7 gather_fusion
  59.3 2.9 %cholesky.194 = f32[32,32]{1,0:T(8,128)S(1)} custom-call(f32[32,32]{1,0:T(8,128)S(1)} %fusion.134), custom_call_target="Cholesky" | custom-call | tf_op jit(solution)/shard_map/jit(cholesky)/cholesky | solution.py:68
  62.3 0.6 compare_reduce_fusion.11
  62.9 0.7 fusion.143
  63.6 2.4 custom-call.34
  67.2 2.9 %cholesky.205 = f32[32,32]{1,0:T(8,128)S(1)} custom-call(f32[32,32]{1,0:T(8,128)S(1)} %fusion.133), custom_call_target="Cholesky" | custom-call | tf_op jit(solution)/shard_map/jit(cholesky)/cholesky | solution.py:36
  70.1 0.6 compare_reduce_fusion.10
  70.8 0.7 fusion.64
  71.4 2.4 custom-call.33
  75.2 0.4 fusion.127
  76.0 0.4 convolution_add_fusion.3
  76.5 3.5 %all-to-all-start.2 = ((bf16[8,4,2048]{2,0,1:T(8,128)(2,1)}), bf16[8,4,2048]{2,0,1:T(8,128)(2,1)S(1)}, u32[]{:S(2)}, u32[]{:S(2)}) async-start(bf16[8,4,2048]{2,0,1:T(8,128)(2,1)} %bitcast.39), calls=%async_computation.2 | async-start | bytes 262144 | tf_op jit(solution)/shard_map/all_to_all | solution.py:49
  80.4 41.5 %all-reduce.6 = (f32[32,32]{0,1:T(8,128)S(1)}, f32[32,32]{0,1:T(8,128)S(1)}) all-reduce(f32[32,32]{0,1:T(8,128)S(1)} %fusion.14, f32[32,32]{0,1:T(8,128)S(1)} %fusion.12), channel_id=1, replica_groups=mesh['rows'=8,'grp'=4] {'rows','grp'}, use_global_device_ids=true, to_apply=%region_5.9 | all-reduce | flops 2048 | bytes 16384 | tf_op jit(solution)/shard_map/psum | solution.py:51
  121.9 0.7 gather_fusion.1
  123.5 2.9 %cholesky.216 = f32[32,32]{1,0:T(8,128)S(1)} custom-call(f32[32,32]{1,0:T(8,128)S(1)} %fusion.129), custom_call_target="Cholesky" | custom-call | tf_op jit(solution)/shard_map/jit(cholesky)/cholesky | solution.py:38
  126.6 0.6 compare_reduce_fusion.9
  127.3 0.6 fusion.163
  128.5 2.9 %cholesky.227 = f32[32,32]{1,0:T(8,128)S(1)} custom-call(f32[32,32]{1,0:T(8,128)S(1)} %fusion.121), custom_call_target="Cholesky" | custom-call | tf_op jit(solution)/shard_map/jit(cholesky)/cholesky | solution.py:68
  131.5 0.6 compare_reduce_fusion.8
  132.1 0.7 fusion.144
  132.8 2.4 custom-call.39
  136.4 2.9 %cholesky.238 = f32[32,32]{1,0:T(8,128)S(1)} custom-call(f32[32,32]{1,0:T(8,128)S(1)} %fusion.120), custom_call_target="Cholesky" | custom-call | tf_op jit(solution)/shard_map/jit(cholesky)/cholesky | solution.py:36
  139.4 0.6 compare_reduce_fusion.7
  140.0 0.7 fusion.65
  140.7 2.4 custom-call.38
  145.2 0.4 convolution_add_fusion.2
  145.7 3.5 %all-to-all-start.3 = ((bf16[8,4,2048]{2,0,1:T(8,128)(2,1)}), bf16[8,4,2048]{2,0,1:T(8,128)(2,1)S(1)}, u32[]{:S(2)}, u32[]{:S(2)}) async-start(bf16[8,4,2048]{2,0,1:T(8,128)(2,1)} %bitcast.63), calls=%async_computation.3 | async-start | bytes 262144 | tf_op jit(solution)/shard_map/all_to_all | solution.py:49
  149.7 40.7 %all-reduce.5 = (f32[32,32]{0,1:T(8,128)S(1)}, f32[32,32]{0,1:T(8,128)S(1)}) all-reduce(f32[32,32]{0,1:T(8,128)S(1)} %fusion.10, f32[32,32]{0,1:T(8,128)S(1)} %fusion.8), channel_id=1, replica_groups=mesh['rows'=8,'grp'=4] {'rows','grp'}, use_global_device_ids=true, to_apply=%region_7.12 | all-reduce | flops 2048 | bytes 16384 | tf_op jit(solution)/shard_map/psum | solution.py:51
  190.4 0.7 gather_fusion.2
  192.0 2.9 %cholesky.249 = f32[32,32]{1,0:T(8,128)S(1)} custom-call(f32[32,32]{1,0:T(8,128)S(1)} %fusion.116), custom_call_target="Cholesky" | custom-call | tf_op jit(solution)/shard_map/jit(cholesky)/cholesky | solution.py:38
  195.1 0.6 compare_reduce_fusion.6
  195.7 0.6 fusion.164
  197.0 2.9 %cholesky.260 = f32[32,32]{1,0:T(8,128)S(1)} custom-call(f32[32,32]{1,0:T(8,128)S(1)} %fusion.108), custom_call_target="Cholesky" | custom-call | tf_op jit(solution)/shard_map/jit(cholesky)/cholesky | solution.py:68
  199.9 0.6 compare_reduce_fusion.5
  200.6 0.7 fusion.142
  201.2 2.4 custom-call.44
  204.8 2.9 %cholesky.271 = f32[32,32]{1,0:T(8,128)S(1)} custom-call(f32[32,32]{1,0:T(8,128)S(1)} %fusion.107), custom_call_target="Cholesky" | custom-call | tf_op jit(solution)/shard_map/jit(cholesky)/cholesky | solution.py:36
  207.8 0.6 compare_reduce_fusion.4
  208.5 0.7 fusion.66
  209.1 2.4 custom-call.43
  213.7 0.4 convolution_add_fusion.1
  214.6 39.8 %all-reduce.4 = (f32[32,32]{0,1:T(8,128)S(1)}, f32[32,32]{0,1:T(8,128)S(1)}) all-reduce(f32[32,32]{0,1:T(8,128)S(1)} %fusion.6, f32[32,32]{0,1:T(8,128)S(1)} %fusion.4), channel_id=1, replica_groups=mesh['rows'=8,'grp'=4] {'rows','grp'}, use_global_device_ids=true, to_apply=%region_9.14 | all-reduce | flops 2048 | bytes 16384 | tf_op jit(solution)/shard_map/psum | solution.py:51
  254.5 0.7 gather_fusion.3
  256.1 2.9 %cholesky.282 = f32[32,32]{1,0:T(8,128)S(1)} custom-call(f32[32,32]{1,0:T(8,128)S(1)} %fusion.103), custom_call_target="Cholesky" | custom-call | tf_op jit(solution)/shard_map/jit(cholesky)/cholesky | solution.py:38
  259.2 0.6 compare_reduce_fusion.3
  259.9 0.6 select_select_fusion.5
  260.8 0.7 copy.105
  261.8 2.9 %cholesky.293 = f32[32,32]{1,0:T(8,128)S(1)} custom-call(f32[32,32]{1,0:T(8,128)S(1)} %fusion.95), custom_call_target="Cholesky" | custom-call | tf_op jit(solution)/shard_map/jit(cholesky)/cholesky | solution.py:68
  264.7 0.6 compare_reduce_fusion.2
  265.4 0.7 select_bitcast_fusion
  266.0 2.4 custom-call.49
  269.0 2.9 %cholesky.304 = f32[32,32]{1,0:T(8,128)S(1)} custom-call(f32[32,32]{1,0:T(8,128)S(1)} %fusion.94), custom_call_target="Cholesky" | custom-call | tf_op jit(solution)/shard_map/jit(cholesky)/cholesky | solution.py:36
  272.0 0.6 compare_reduce_fusion.1
  272.6 0.7 fusion.67
  273.3 2.4 custom-call.48
  276.5 2.9 %cholesky.315 = f32[32,32]{1,0:T(8,128)S(1)} custom-call(f32[32,32]{1,0:T(8,128)S(1)} %fusion.88), custom_call_target="Cholesky" | custom-call | tf_op jit(solution)/shard_map/jit(cholesky)/cholesky | solution.py:38
  279.4 0.6 compare_reduce_fusion
  280.1 1.3 select_select_fusion.4
  282.5 1.1 convolution_add_fusion
  (138 shorter events, 20.1 us)
Async XLA Ops:
  0.6 6.4 %copy-start = (f32[32,2048]{1,0:T(8,128)S(1)}, f32[32,2048]{1,0:T(8,128)}, u32[]{:S(2)}) copy-start(f32[32,2048]{1,0:T(8,128)} %param.10) | copy-start | bytes 786436
  2.6 4.4 %copy-start.1 = (f32[32,32]{1,0:T(8,128)S(1)}, f32[32,32]{1,0:T(8,128)}, u32[]{:S(2)}) copy-start(f32[32,32]{1,0:T(8,128)} %param.11) | copy-start | bytes 12292
  2.6 9.0 %all-to-all-start = ((bf16[8,4,2048]{2,0,1:T(8,128)(2,1)}), bf16[8,4,2048]{2,0,1:T(8,128)(2,1)S(1)}, u32[]{:S(2)}, u32[]{:S(2)}) async-start(bf16[8,4,2048]{2,0,1:T(8,128)(2,1)} %bitcast), calls=%async_computation | async-start | bytes 262144 | tf_op jit(solution)/shard_map/all_to_all | solution.py:49
  11.6 64.9 %all-to-all-start.1 = ((bf16[8,4,2048]{2,0,1:T(8,128)(2,1)}), bf16[8,4,2048]{2,0,1:T(8,128)(2,1)S(1)}, u32[]{:S(2)}, u32[]{:S(2)}) async-start(bf16[8,4,2048]{2,0,1:T(8,128)(2,1)} %bitcast.15), calls=%async_computation.1 | async-start | bytes 262144 | tf_op jit(solution)/shard_map/all_to_all | solution.py:49
  76.5 69.2 %all-to-all-start.2 = ((bf16[8,4,2048]{2,0,1:T(8,128)(2,1)}), bf16[8,4,2048]{2,0,1:T(8,128)(2,1)S(1)}, u32[]{:S(2)}, u32[]{:S(2)}) async-start(bf16[8,4,2048]{2,0,1:T(8,128)(2,1)} %bitcast.39), calls=%async_computation.2 | async-start | bytes 262144 | tf_op jit(solution)/shard_map/all_to_all | solution.py:49
  145.7 68.5 %all-to-all-start.3 = ((bf16[8,4,2048]{2,0,1:T(8,128)(2,1)}), bf16[8,4,2048]{2,0,1:T(8,128)(2,1)S(1)}, u32[]{:S(2)}, u32[]{:S(2)}) async-start(bf16[8,4,2048]{2,0,1:T(8,128)(2,1)} %bitcast.63), calls=%async_computation.3 | async-start | bytes 262144 | tf_op jit(solution)/shard_map/all_to_all | solution.py:49
where the time goes:
time: 285 us; the launch traced here: 284 us
  blocking collectives  164 us (58%)
  other arithmetic  71.8 us (25%)
  matrix products  20.3 us (7%)
  starting transfers between devices  14.7 us (5%)
  local copies, waits for them, and re-layouts  7.12 us (2%)
  waiting for transfers between devices  4.15 us (1%)
    psum x3, blocking collectives, body(): lax.psum((contract_rows(basis_now, raw), contract_rows(raw, raw)), ('rows...  122 us
    psum x1, blocking collectives, body(): gram_basis = lax.psum(contract_rows(basis_now, basis_now), ('rows', 'grp'))  42.1 us
    another operation x16, other arithmetic, lower_solve(): lax.linalg.triangular_solve(factor, right, left_side=True, lower=True)  24.7 us
    all_to_all x4, starting transfers between devices, body(): lax.all_to_all(snapshots[batch], 'grp', split_axis=1, concat_axis=0, tile...  14.7 us
    another operation x12, other arithmetic, small_update(): jnp.linalg.cholesky(matmul(rotation.T, matmul(moment, rotation)))  14.7 us
    another operation x12, other arithmetic, small_update(): factor = jnp.linalg.cholesky(matmul(leading.T, leading))  14.4 us
    another operation x12, other arithmetic, body(): lower = jnp.linalg.cholesky(gram)  14.4 us
    dot_general x54, matrix products, matmul(): jnp.dot(left, right, precision=lax.Precision.HIGHEST, preferred_element_t...  13.7 us
  transfers between devices with their start and end apart: 4, of which 1 were waited for; matrix products, arithmetic and copies ran while one was open for 24% of the time, Pallas kernels for 0%

commit v1 on v0

--- a/solution.py
+++ b/solution.py
@@ -44,7 +44,9 @@
     basis_now = basis
     core_now = core
     firsts = []
-    gram_basis = lax.psum(contract_rows(basis_now, basis_now), ("rows", "grp"))
+    gram_basis = contract_rows(basis_now, basis_now)
+    for axis in ("grp", "rows"):
+        gram_basis = lax.psum(gram_basis, axis)
     for batch in range(BATCHES):
         columns = lax.all_to_all(snapshots[batch], "grp", split_axis=1, concat_axis=0, tiled=True)
         raw = columns.astype(jnp.float32)

time: 285 us -> 327 us (1.15)
  blocking collectives: 164 us -> 210 us
  waiting for transfers between devices: 4.15 us -> 0.01 us
    psum x3 -> x4, blocking collectives: 122 us -> 161 us  [body(): lax.psum((contract_rows(basis_now, raw), contract_rows(raw, raw)), ('rows...]
    psum x1 -> x2, blocking collectives: 42.1 us -> 49.6 us  [body(): gram_basis = lax.psum(gram_basis, axis)]
    all_to_all x4, waiting for transfers between devices: 4.15 us -> 0.01 us  [body(): lax.all_to_all(snapshots[batch], 'grp', split_axis=1, concat_axis=0, tile...]
  transfers between devices with their start and end apart: 4 -> 4, of which waited for: 1 -> 0; matrix products, arithmetic and copies ran while one was open for 24% -> 21% of each run, Pallas kernels for 0% -> 0%
where the time goes in v1:
time: 327 us; the launch traced here: 326 us
  blocking collectives  210 us (64%)
  other arithmetic  71.8 us (22%)
  matrix products  20.2 us (6%)
  starting transfers between devices  14.8 us (5%)
  local copies, waits for them, and re-layouts  7.12 us (2%)
    psum x4, blocking collectives, body(): lax.psum((contract_rows(basis_now, raw), contract_rows(raw, raw)), ('rows...  161 us
    psum x2, blocking collectives, body(): gram_basis = lax.psum(gram_basis, axis)  49.6 us
    another operation x16, other arithmetic, lower_solve(): lax.linalg.triangular_solve(factor, right, left_side=True, lower=True)  24.7 us
    all_to_all x4, starting transfers between devices, body(): lax.all_to_all(snapshots[batch], 'grp', split_axis=1, concat_axis=0, tile...  14.8 us
    another operation x12, other arithmetic, small_update(): jnp.linalg.cholesky(matmul(rotation.T, matmul(moment, rotation)))  14.7 us
    another operation x12, other arithmetic, small_update(): factor = jnp.linalg.cholesky(matmul(leading.T, leading))  14.4 us
    another operation x12, other arithmetic, body(): lower = jnp.linalg.cholesky(gram)  14.4 us
    dot_general x54, matrix products, matmul(): jnp.dot(left, right, precision=lax.Precision.HIGHEST, preferred_element_t...  13.7 us
  transfers between devices with their start and end apart: 4, of which 0 were waited for; matrix products, arithmetic and copies ran while one was open for 21% of the time, Pallas kernels for 0%

profile of v1, /device:TPU:0, one launch (start us, length us, event | category | flops | bytes accessed | tf_op | source)
XLA Modules:
  0.0 325.5 jit_solution(11065912709965749365)
XLA Ops:
  0.6 1.9 fusion.229
  2.6 4.4 %all-to-all-start = ((bf16[8,4,2048]{2,0,1:T(8,128)(2,1)}), bf16[8,4,2048]{2,0,1:T(8,128)(2,1)S(1)}, u32[]{:S(2)}, u32[]{:S(2)}) async-start(bf16[8,4,2048]{2,0,1:T(8,128)(2,1)} %bitcast), calls=%async_computation | async-start | bytes 262144 | tf_op jit(solution)/shard_map/all_to_all | solution.py:51
  7.4 11.8 %psum.72 = f32[32,32]{1,0:T(8,128)S(1)} all-reduce(f32[32,32]{1,0:T(8,128)S(1)} %fusion.230), channel_id=1, replica_groups=mesh['rows'=8,'grp'=4] {'grp'}, use_global_device_ids=true, to_apply=%region_2.0 | all-reduce | flops 1024 | bytes 8192 | tf_op jit(solution)/shard_map/psum | solution.py:49
  19.1 37.9 %psum.73 = f32[32,32]{1,0:T(8,128)S(1)} all-reduce(f32[32,32]{1,0:T(8,128)S(1)} %psum.72), channel_id=1, replica_groups=mesh['rows'=8,'grp'=4] {'rows'}, use_global_device_ids=true, to_apply=%region_3.0 | all-reduce | flops 1024 | bytes 8192 | tf_op jit(solution)/shard_map/psum | solution.py:49
  57.0 3.3 %all-to-all-start.1 = ((bf16[8,4,2048]{2,0,1:T(8,128)(2,1)}), bf16[8,4,2048]{2,0,1:T(8,128)(2,1)S(1)}, u32[]{:S(2)}, u32[]{:S(2)}) async-start(bf16[8,4,2048]{2,0,1:T(8,128)(2,1)} %bitcast.15), calls=%async_computation.1 | async-start | bytes 262144 | tf_op jit(solution)/shard_map/all_to_all | solution.py:51
  60.8 37.2 %all-reduce.7 = (f32[32,32]{0,1:T(8,128)S(1)}, f32[32,32]{0,1:T(8,128)S(1)}) all-reduce(f32[32,32]{0,1:T(8,128)S(1)} %fusion.18, f32[32,32]{0,1:T(8,128)S(1)} %fusion.16), channel_id=1, replica_groups=mesh['rows'=8,'grp'=4] {'rows','grp'}, use_global_device_ids=true, to_apply=%region_0.0 | all-reduce | flops 2048 | bytes 16384 | tf_op jit(solution)/shard_map/psum | solution.py:53
  98.0 0.7 gather_fusion
  99.9 2.9 cholesky.194
  102.9 0.6 compare_reduce_fusion.11
  103.5 0.7 fusion.143
  104.2 2.4 custom-call.34
  107.8 2.9 cholesky.205
  110.7 0.6 compare_reduce_fusion.10
  111.4 0.7 fusion.64
  112.0 2.4 custom-call.33
  116.6 0.4 convolution_add_fusion.3
  117.1 3.5 %all-to-all-start.2 = ((bf16[8,4,2048]{2,0,1:T(8,128)(2,1)}), bf16[8,4,2048]{2,0,1:T(8,128)(2,1)S(1)}, u32[]{:S(2)}, u32[]{:S(2)}) async-start(bf16[8,4,2048]{2,0,1:T(8,128)(2,1)} %bitcast.39), calls=%async_computation.2 | async-start | bytes 262144 | tf_op jit(solution)/shard_map/all_to_all | solution.py:51
  121.1 42.8 %all-reduce.6 = (f32[32,32]{0,1:T(8,128)S(1)}, f32[32,32]{0,1:T(8,128)S(1)}) all-reduce(f32[32,32]{0,1:T(8,128)S(1)} %fusion.14, f32[32,32]{0,1:T(8,128)S(1)} %fusion.12), channel_id=1, replica_groups=mesh['rows'=8,'grp'=4] {'rows','grp'}, use_global_device_ids=true, to_apply=%region_6.10 | all-reduce | flops 2048 | bytes 16384 | tf_op jit(solution)/shard_map/psum | solution.py:53
  163.9 0.7 gather_fusion.1
  165.5 2.9 cholesky.216
  168.6 0.6 compare_reduce_fusion.9
  169.2 0.6 fusion.163
  170.5 2.9 cholesky.227
  173.4 0.6 compare_reduce_fusion.8
  174.1 0.7 fusion.144
  174.7 2.4 custom-call.39
  178.3 2.9 cholesky.238
  181.3 0.6 compare_reduce_fusion.7
  182.0 0.7 fusion.65
  182.6 2.4 custom-call.38
  187.2 0.4 convolution_add_fusion.2
  187.7 3.5 %all-to-all-start.3 = ((bf16[8,4,2048]{2,0,1:T(8,128)(2,1)}), bf16[8,4,2048]{2,0,1:T(8,128)(2,1)S(1)}, u32[]{:S(2)}, u32[]{:S(2)}) async-start(bf16[8,4,2048]{2,0,1:T(8,128)(2,1)} %bitcast.63), calls=%async_computation.3 | async-start | bytes 262144 | tf_op jit(solution)/shard_map/all_to_all | solution.py:51
  191.6 40.1 %all-reduce.5 = (f32[32,32]{0,1:T(8,128)S(1)}, f32[32,32]{0,1:T(8,128)S(1)}) all-reduce(f32[32,32]{0,1:T(8,128)S(1)} %fusion.10, f32[32,32]{0,1:T(8,128)S(1)} %fusion.8), channel_id=1, replica_groups=mesh['rows'=8,'grp'=4] {'rows','grp'}, use_global_device_ids=true, to_apply=%region_8.13 | all-reduce | flops 2048 | bytes 16384 | tf_op jit(solution)/shard_map/psum | solution.py:53
  231.7 0.7 gather_fusion.2
  233.3 2.9 cholesky.249
  236.4 0.6 compare_reduce_fusion.6
  237.1 0.6 fusion.164
  238.3 2.9 cholesky.260
  241.3 0.6 compare_reduce_fusion.5
  241.9 0.7 fusion.142
  242.6 2.4 custom-call.44
  246.2 2.9 cholesky.271
  249.1 0.6 compare_reduce_fusion.4
  249.8 0.7 fusion.66
  250.4 2.4 custom-call.43
  255.0 0.4 convolution_add_fusion.1
  255.9 40.5 %all-reduce.4 = (f32[32,32]{0,1:T(8,128)S(1)}, f32[32,32]{0,1:T(8,128)S(1)}) all-reduce(f32[32,32]{0,1:T(8,128)S(1)} %fusion.6, f32[32,32]{0,1:T(8,128)S(1)} %fusion.4), channel_id=1, replica_groups=mesh['rows'=8,'grp'=4] {'rows','grp'}, use_global_device_ids=true, to_apply=%region_10.15 | all-reduce | flops 2048 | bytes 16384 | tf_op jit(solution)/shard_map/psum | solution.py:53
  296.4 0.7 gather_fusion.3
  298.0 2.9 cholesky.282
  301.2 0.6 compare_reduce_fusion.3
  301.8 0.6 select_select_fusion.5
  302.7 0.7 copy.105
  303.7 2.9 cholesky.293
  306.7 0.6 compare_reduce_fusion.2
  307.3 0.7 select_bitcast_fusion
  308.0 2.4 custom-call.49
  311.0 2.9 cholesky.304
  313.9 0.6 compare_reduce_fusion.1
  314.6 0.7 fusion.67
  315.2 2.4 custom-call.48
  318.4 2.9 cholesky.315
  321.3 0.6 compare_reduce_fusion
  322.0 1.3 select_select_fusion.4
  324.4 1.1 convolution_add_fusion
  (140 shorter events, 20.5 us)
Async XLA Ops:
  0.6 6.4 %copy-start = (f32[32,2048]{1,0:T(8,128)S(1)}, f32[32,2048]{1,0:T(8,128)}, u32[]{:S(2)}) copy-start(f32[32,2048]{1,0:T(8,128)} %param.10) | copy-start | bytes 786436
  2.6 4.4 %copy-start.1 = (f32[32,32]{1,0:T(8,128)S(1)}, f32[32,32]{1,0:T(8,128)}, u32[]{:S(2)}) copy-start(f32[32,32]{1,0:T(8,128)} %param.11) | copy-start | bytes 12292
  2.6 54.5 %all-to-all-start = ((bf16[8,4,2048]{2,0,1:T(8,128)(2,1)}), bf16[8,4,2048]{2,0,1:T(8,128)(2,1)S(1)}, u32[]{:S(2)}, u32[]{:S(2)}) async-start(bf16[8,4,2048]{2,0,1:T(8,128)(2,1)} %bitcast), calls=%async_computation | async-start | bytes 262144 | tf_op jit(solution)/shard_map/all_to_all | solution.py:51
  57.0 60.0 %all-to-all-start.1 = ((bf16[8,4,2048]{2,0,1:T(8,128)(2,1)}), bf16[8,4,2048]{2,0,1:T(8,128)(2,1)S(1)}, u32[]{:S(2)}, u32[]{:S(2)}) async-start(bf16[8,4,2048]{2,0,1:T(8,128)(2,1)} %bitcast.15), calls=%async_computation.1 | async-start | bytes 262144 | tf_op jit(solution)/shard_map/all_to_all | solution.py:51
  117.1 70.6 %all-to-all-start.2 = ((bf16[8,4,2048]{2,0,1:T(8,128)(2,1)}), bf16[8,4,2048]{2,0,1:T(8,128)(2,1)S(1)}, u32[]{:S(2)}, u32[]{:S(2)}) async-start(bf16[8,4,2048]{2,0,1:T(8,128)(2,1)} %bitcast.39), calls=%async_computation.2 | async-start | bytes 262144 | tf_op jit(solution)/shard_map/all_to_all | solution.py:51
  187.7 67.8 %all-to-all-start.3 = ((bf16[8,4,2048]{2,0,1:T(8,128)(2,1)}), bf16[8,4,2048]{2,0,1:T(8,128)(2,1)S(1)}, u32[]{:S(2)}, u32[]{:S(2)}) async-start(bf16[8,4,2048]{2,0,1:T(8,128)(2,1)} %bitcast.63), calls=%async_computation.3 | async-start | bytes 262144 | tf_op jit(solution)/shard_map/all_to_all | solution.py:51
